TPU v7x, 32 devices: a whole 2x2x4 slice. The times are simulated.
32 devices in a mesh: px: 8 (over z, y), py: 4 (over x, core).
Axes of the slice: x: 2, y: 2, z: 4, core: 2. Of those that a mesh axis runs over, the one named last changes fastest.
Arguments:
- field: bfloat16 [1, 32, 128, 128, 256], P(None, None, 'px', 'py'), may hold values from -6 to 6
- spectral_weight: bfloat16 [2, 32, 32, 32, 64, 64], P(None, None, 'px', 'py'), may hold values from -72 to 72
- point_weight: bfloat16 [32, 32], replicated, may hold values from -1 to 1
- point_bias: float32 [32], replicated, may hold values from -3 to 3
Outputs:
- layer_out: bfloat16 [1, 32, 128, 128, 256], P(None, None, 'px', 'py')
All inputs are finite; a program needn't handle non-finite values.
Results may differ from a plain program's by a relative error of at most 0.0085.
Values may be sent and summed in bfloat16 or wider, within the bound.
A program may use at most 192 MiB of HBM per device.

v0:
```python
from functools import partial
import math

import jax
import jax.numpy as jnp
from jax import lax
from jax.sharding import PartitionSpec as P

MX = 64
MY = 64
MZ = 32


def contract(form, left, right):
    return jnp.einsum(
        form, left, right, precision=lax.Precision.HIGHEST, preferred_element_type=jnp.float32
    )


def angle_table(length, count, signed):
    position = jnp.arange(length, dtype=jnp.int32)
    number = jnp.arange(count, dtype=jnp.int32)
    if signed:
        number = jnp.where(number < count // 2, number, number - count)
    product = position[:, None] * number[None, :] % length
    return 2.0 * math.pi / length * product.astype(jnp.float32)


def forward_x(piece, keep_count, cos_x, sin_x):
    real_part = piece[0]
    imag_part = piece[1]
    out_real = contract("ix,bcxm->bcim", cos_x, real_part) + contract(
        "ix,bcxm->bcim", sin_x, imag_part
    )
    out_imag = contract("ix,bcxm->bcim", cos_x, imag_part) - contract(
        "ix,bcxm->bcim", sin_x, real_part
    )
    return jnp.stack([out_real, out_imag], axis=0)


def inverse_z(piece, table):
    return contract("pbcxky,pkz->bcxyz", piece, table)


def body(field, spectral_weight, point_weight, point_bias):
    batch, channels, rows_x, rows_y, depth = field.shape
    grid_x = rows_x * lax.axis_size("px")
    grid_y = rows_y * lax.axis_size("py")
    theta_x = angle_table(grid_x, MX, True)
    theta_y = angle_table(grid_y, MY, True)
    wide = field.astype(jnp.float32)
    count = MZ
    theta_z = angle_table(depth, count, False)
    z_real = contract("bcxyz,zk->bcxky", wide, jnp.cos(theta_z))
    z_imag = contract("bcxyz,zk->bcxky", wide, -jnp.sin(theta_z))
    along_z = jnp.stack([z_real, z_imag], axis=0).reshape(
        2, batch, channels, rows_x, count * rows_y
    )
    step_x = partial(
        forward_x, keep_count=MZ * rows_y, cos_x=jnp.cos(theta_x).T, sin_x=jnp.sin(theta_x).T
    )
    along_x = step_x(lax.all_to_all(along_z, "px", split_axis=2, concat_axis=3, tiled=True))
    shape = along_x.shape
    along_x = along_x.reshape(shape[0], shape[1], shape[2], shape[3], MZ, rows_y)
    moved = lax.all_to_all(along_x, "py", split_axis=4, concat_axis=5, tiled=True)
    cos_y = jnp.cos(theta_y)
    sin_y = jnp.sin(theta_y)
    spec_real = contract("bciky,yj->bcikj", moved[0], cos_y) + contract(
        "bciky,yj->bcikj", moved[1], sin_y
    )
    spec_imag = contract("bciky,yj->bcikj", moved[1], cos_y) - contract(
        "bciky,yj->bcikj", moved[0], sin_y
    )
    spectrum = jnp.stack([spec_real, spec_imag], axis=0).astype(jnp.bfloat16)
    gathered = lax.all_gather(spectrum, "px", axis=2, tiled=True)
    in_real = gathered[0].astype(jnp.float32)
    in_imag = gathered[1].astype(jnp.float32)
    weight_real = spectral_weight[0].astype(jnp.float32)
    weight_imag = spectral_weight[1].astype(jnp.float32)
    mixed_real = contract("bcikj,cokij->boikj", in_real, weight_real) - contract(
        "bcikj,cokij->boikj", in_imag, weight_imag
    )
    mixed_imag = contract("bcikj,cokij->boikj", in_real, weight_imag) + contract(
        "bcikj,cokij->boikj", in_imag, weight_real
    )
    cos_yt = jnp.cos(theta_y).T
    sin_yt = jnp.sin(theta_y).T
    back_real = contract("boikj,jy->boiky", mixed_real, cos_yt) - contract(
        "boikj,jy->boiky", mixed_imag, sin_yt
    )
    back_imag = contract("boikj,jy->boiky", mixed_real, sin_yt) + contract(
        "boikj,jy->boiky", mixed_imag, cos_yt
    )
    returned = lax.all_to_all(
        jnp.stack([back_real, back_imag], axis=0), "py", split_axis=5, concat_axis=4, tiled=True
    )
    cos_xt = jnp.cos(theta_x)
    sin_xt = jnp.sin(theta_x)
    out_real = contract("xi,boiky->boxky", cos_xt, returned[0]) - contract(
        "xi,boiky->boxky", sin_xt, returned[1]
    )
    out_imag = contract("xi,boiky->boxky", sin_xt, returned[0]) + contract(
        "xi,boiky->boxky", cos_xt, returned[1]
    )
    planes = jnp.stack([out_real, out_imag], axis=0)
    theta_back = angle_table(depth, MZ, False).T
    factor = jnp.where(jnp.arange(MZ) == 0, 1.0, 2.0).astype(jnp.float32) / float(
        grid_x * grid_y * depth
    )
    table_back = jnp.stack(
        [factor[:, None] * jnp.cos(theta_back), -factor[:, None] * jnp.sin(theta_back)], axis=0
    )
    spectral = inverse_z(
        lax.all_to_all(planes, "px", split_axis=3, concat_axis=2, tiled=True), table=table_back
    )
    pointwise = jnp.einsum(
        "oc,bcxyz->boxyz", point_weight, field, preferred_element_type=jnp.float32
    )
    pointwise = pointwise + point_bias[None, :, None, None, None]
    return jax.nn.gelu(spectral + pointwise, approximate=False).astype(jnp.bfloat16)


def solution(mesh):
    placed = (P(None, None, "px", "py", None), P(None, None, "px", "py", None, None), P(), P())
    return jax.shard_map(
        body, mesh=mesh, in_specs=placed, out_specs=P(None, None, "px", "py", None), check_vma=False
    )
```

profile of v0, /device:TPU:15, one launch (start us, length us, event | category | flops | bytes accessed | tf_op | source)
XLA Modules:
  0.0 741.3 jit_solution(797422356262062606)
XLA Ops:
  6.5 24.2 %convolution_bitcast_fusion.1 = f32[1,32,16,32,32]{4,3,2,1,0:T(8,128)} fusion(bf16[1,32,16,32,256]{4,3,2,1,0:T(8,128)(2,1)} %param.4), kind=kOutput, calls=%fused_computation.41 | convolution fusion | flops 1610727424 | bytes 10485760 | tf_op jit(solution)/shard_map/bcxyz,zk->bcxky/dot_general | solution.py:15
  30.8 21.1 %convolution_bitcast_fusion = f32[1,32,16,32,32]{4,3,2,1,0:T(8,128)} fusion(bf16[1,32,16,32,256]{4,3,2,1,0:T(8,128)(2,1)S(1)} %copy-done.2), kind=kOutput, calls=%fused_computation.40 | convolution fusion | flops 1610735616 | bytes 10485760 | tf_op jit(solution)/shard_map/bcxyz,zk->bcxky/dot_general | solution.py:15
  51.9 6.6 stack.50
  58.6 7.9 %stack.51 = f32[1,1,32,16,1024]{4,3,2,1,0:T(8,128)} reshape(f32[1,32,16,32,32]{4,3,2,1,0:T(8,128)} %convolution_bitcast_fusion) | data formatting | bytes 4194304 | tf_op jit(solution)/shard_map/stack | solution.py:56
  70.8 5.7 all-to-all-start
  76.5 90.6 %all-to-all-done = f32[2,1,32,16,1024]{4,3,1,0,2:T(8,128)} async-done(((f32[2,1,32,16,1024]{4,3,1,0,2:T(8,128)}), f32[2,1,32,16,1024]{4,3,1,0,2:T(8,128)}, u32[]{:S(2)}, u32[]{:S(2)}) %all-to-all-start) | async-done | bytes 4194336 | tf_op jit(solution)/shard_map/all_to_all | solution.py:62
  190.2 27.7 %all_to_all.60 = f32[4,1,131072]{2,1,0:T(1,128)} all-to-all(f32[4,1,131072]{2,1,0:T(1,128)S(1)} %reshape.325), channel_id=1, replica_groups=mesh['px'=8,'py'=4] {'py'}, dimensions={0} | all-to-all | bytes 4194304 | tf_op jit(solution)/shard_map/all_to_all | solution.py:65
  218.4 7.7 %reduce.8 = f32[4,131072]{1,0:T(4,128)S(1)} reduce(f32[4,1,131072]{2,1,0:T(1,128)} %all_to_all.60, f32[]{:T(128)} %broadcast.331), dimensions={1}, to_apply=%all_to_all.47.reduce_sub_computation | reduce | bytes 4194308 | tf_op jit(solution)/shard_map/all_to_all | solution.py:65
  243.9 123.1 %all-gather.2.cloned.1.call-done = bf16[2,1,32,64,8,64]{5,4,3,2,1,0:T(8,128)(2,1)} async-done(((bf16[2,1,4,64,8,64]{5,4,3,2,1,0:T(8,128)(2,1)}), bf16[2,1,32,64,8,64]{5,4,3,2,1,0:T(8,128)(2,1)}) %all-gather.2.cloned.1.call-update) | async-done | bytes 4194320 | tf_op jit(solution)/shard_map/all_gather | solution.py:75
  367.0 11.7 %fusion.16 = (f32[64,8,64,32]{2,1,0,3:T(8,128)}, f32[64,8,64,32]{2,1,0,3:T(8,128)}) fusion(bf16[2,1,32,64,8,64]{5,4,3,2,1,0:T(8,128)(2,1)} %all-gather.2.cloned.1.call-done), kind=kLoop, calls=%fused_computation.32 | loop fusion | flops 2097152 | bytes 12582912
  378.7 8.4 %copy.107 = f32[64,8,64,32]{2,0,1,3:T(8,128)} copy(f32[64,8,64,32]{2,1,0,3:T(8,128)} %get-tuple-element.11) | data formatting | bytes 8388608
  392.1 23.1 %fusion.3 = (f32[64,8,64,4]{2,0,1,3:T(8,128)S(1)}, f32[64,8,64,4]{2,0,1,3:T(8,128)S(1)}, f32[64,8,64,4]{2,0,1,3:T(8,128)}, f32[64,8,64,4]{2,0,1,3:T(8,128)S(1)}) fusion(f32[64,8,64,32]{2,0,1,3:T(8,128)} %copy.106, bf16[2,32,4,8,64,64]{5,4,3,2,1,0:T(8,128)(2,1)} %param.5, f32[64,8,64,32]{2,0,1,3:T(8,128)} %copy.107), kind=kLoop, calls=%fused_computation.7 | loop fusion | flops 41418752 | bytes 27262976
  436.9 28.6 %all_to_all.61 = f32[4,1,131072]{2,1,0:T(1,128)} all-to-all(f32[4,1,131072]{2,1,0:T(1,128)S(1)} %reshape.327), channel_id=1, replica_groups=mesh['px'=8,'py'=4] {'py'}, dimensions={0} | all-to-all | bytes 4194304 | tf_op jit(solution)/shard_map/all_to_all | solution.py:94
  465.5 7.7 %reduce.9 = f32[4,131072]{1,0:T(4,128)S(1)} reduce(f32[4,1,131072]{2,1,0:T(1,128)} %all_to_all.61, f32[]{:T(128)} %broadcast.331), dimensions={1}, to_apply=%all_to_all.50.reduce_sub_computation | reduce | bytes 4194308 | tf_op jit(solution)/shard_map/all_to_all | solution.py:94
  494.2 14.4 %copy.62 = f32[2,1,4,128,32,32]{5,4,2,1,0,3:T(8,128)} copy(f32[2,1,4,128,32,32]{3,5,4,2,1,0:T(8,128)} %pad_maximum_fusion.2) | data formatting | bytes 8388608 | tf_op jit(solution)/shard_map/stack | solution.py:105
  508.6 12.8 %reshape.329 = f32[8,1,131072]{2,1,0:T(1,128)} reshape(f32[128,2,1,4,32,32]{5,4,3,2,1,0:T(8,128)} %bitcast.215) | data formatting | bytes 8388608
  521.4 7.7 %all-to-all-start.3 = ((f32[8,1,131072]{2,1,0:T(1,128)}), f32[8,1,131072]{2,1,0:T(1,128)}, u32[]{:S(2)}, u32[]{:S(2)}) async-start(f32[8,1,131072]{2,1,0:T(1,128)} %reshape.329), calls=%async_computation.3 | async-start | bytes 8388608 | tf_op jit(solution)/shard_map/all_to_all | solution.py:114
  529.4 14.2 %fusion.14 = f32[16,32,256,32]{2,3,1,0:T(8,128)} fusion(bf16[32,16,32,256]{3,2,1,0:T(8,128)(2,1)} %bitcast.214, bf16[32,32]{1,0:T(8,128)(2,1)S(1)} %copy-done), kind=kOutput, calls=%fused_computation.29 | convolution fusion | flops 268435456 | bytes 25167872 | tf_op jit(solution)/shard_map/oc,bcxyz->boxyz/dot_general | solution.py:116
  543.6 76.2 %all-to-all-done.3 = f32[8,1,131072]{2,1,0:T(1,128)} async-done(((f32[8,1,131072]{2,1,0:T(1,128)}), f32[8,1,131072]{2,1,0:T(1,128)}, u32[]{:S(2)}, u32[]{:S(2)}) %all-to-all-start.3) | async-done | bytes 4194336 | tf_op jit(solution)/shard_map/all_to_all | solution.py:114
  619.7 14.9 %reduce.10 = f32[8,131072]{1,0:T(8,128)} reduce(f32[8,1,131072]{2,1,0:T(1,128)} %all-to-all-done.3, f32[]{:T(128)} %broadcast.331), dimensions={1}, to_apply=%all_to_all.53.reduce_sub_computation | reduce | bytes 8388612 | tf_op jit(solution)/shard_map/all_to_all | solution.py:114
  634.7 13.3 %reshape.330 = f32[128,2,1,4,32,32]{5,4,3,2,1,0:T(8,128)} reshape(f32[8,131072]{1,0:T(8,128)} %reduce.10) | data formatting | bytes 8388608
  648.0 11.8 %copy.63 = f32[2,1,4,128,32,32]{5,4,3,2,0,1:T(8,128)} copy(f32[2,1,4,128,32,32]{5,4,2,1,0,3:T(8,128)} %bitcast.216) | data formatting | bytes 8388608 | tf_op jit(solution)/shard_map/all_to_all | solution.py:114
  659.8 16.4 %copy.64 = f32[2,1,8,4,16,32,32]{5,6,0,4,3,2,1:T(8,128)} copy(f32[2,1,8,4,16,32,32]{6,5,4,2,3,0,1:T(8,128)} %bitcast.217) | data formatting | bytes 8388608 | tf_op jit(solution)/shard_map/all_to_all | solution.py:114
  676.2 57.7 %fusion.6 = bf16[1,32,16,32,256]{4,3,2,1,0:T(8,128)(2,1)} fusion(f32[16,32,256,32]{2,3,1,0:T(8,128)} %fusion.14, f32[2,32,16,32,32]{3,4,0,2,1:T(8,128)} %bitcast.227, f32[32]{0:T(128)S(1)} %copy-done.4, f32[1,32,256]{2,1,0:T(8,128)S(1)} %get-tuple-element.19, f32[1,32,256]{2,1,0:T(8,128)S(1)} %get-tuple-element.20), kind=kOutput, calls=%fused_computation.11 | convolution fusion | flops 3502260224 | bytes 29425792 | tf_op jit(solution)/shard_map/pbcxky,pkz->bcxyz/dot_general | solution.py:15
  (56 shorter events, 93.5 us)
Async XLA Ops:
  6.5 522.8 %copy-start = (bf16[32,32]{1,0:T(8,128)(2,1)S(1)}, bf16[32,32]{1,0:T(8,128)(2,1)}, u32[]{:S(2)}) copy-start(bf16[32,32]{1,0:T(8,128)(2,1)} %param.6) | copy-start | bytes 6148
  6.5 24.2 %copy-start.2 = (bf16[1,32,16,32,256]{4,3,2,1,0:T(8,128)(2,1)S(1)}, bf16[1,32,16,32,256]{4,3,2,1,0:T(8,128)(2,1)}, u32[]{:S(2)}) copy-start(bf16[1,32,16,32,256]{4,3,2,1,0:T(8,128)(2,1)} %param.4) | copy-start | bytes 25165828
  70.8 96.3 %all-to-all-start = ((f32[2,1,32,16,1024]{4,3,1,0,2:T(8,128)}), f32[2,1,32,16,1024]{4,3,1,0,2:T(8,128)}, u32[]{:S(2)}, u32[]{:S(2)}) async-start(f32[2,1,32,16,1024]{4,3,1,0,2:T(8,128)} %pad_maximum_fusion), calls=%async_computation | async-start | bytes 8388608 | tf_op jit(solution)/shard_map/all_to_all | solution.py:62
  76.5 290.5 %all-gather.2.cloned.1.call-start = ((), (), s32[]{:S(2)}) async-start(), calls=%async_computation.4 | async-start | bytes 9437184 | tf_op jit(solution)/shard_map/all_gather | solution.py:75
  378.7 8.4 %copy-start.3 = (f32[64,8,64,32]{2,1,0,3:T(8,128)S(1)}, f32[64,8,64,32]{2,1,0,3:T(8,128)}, u32[]{:S(2)}) copy-start(f32[64,8,64,32]{2,1,0,3:T(8,128)} %get-tuple-element.12) | copy-start | bytes 12582916
  521.4 98.3 %all-to-all-start.3 = ((f32[8,1,131072]{2,1,0:T(1,128)}), f32[8,1,131072]{2,1,0:T(1,128)}, u32[]{:S(2)}, u32[]{:S(2)}) async-start(f32[8,1,131072]{2,1,0:T(1,128)} %reshape.329), calls=%async_computation.3 | async-start | bytes 8388608 | tf_op jit(solution)/shard_map/all_to_all | solution.py:114
  659.8 16.4 %copy-start.4 = (f32[32]{0:T(128)S(1)}, f32[32]{0:T(128)}, u32[]{:S(2)}) copy-start(f32[32]{0:T(128)} %param.7) | copy-start | bytes 388
  676.2 57.7 %copy-start.1 = (bf16[32,32]{1,0:T(8,128)(2,1)S(1)}, bf16[32,32]{1,0:T(8,128)(2,1)}, u32[]{:S(2)}) copy-start(bf16[32,32]{1,0:T(8,128)(2,1)} %param.6) | copy-start | bytes 6148
Sparse Core Ops, SparseCore 0:
  244.0 122.9 all-gather.1
where the time goes:
time: 756 us; the launch traced here: 741 us
  waiting for transfers between devices  290 us (38%)
  matrix products  150 us (20%)
  local copies, waits for them, and re-layouts  139 us (18%)
  other arithmetic  78.1 us (10%)
  blocking collectives  56.2 us (7%)
  between operations  14.2 us (2%)
  starting transfers between devices  13.4 us (2%)
    dot_general x19, matrix products, contract(): jnp.einsum(form, left, right, precision=lax.Precision.HIGHEST, preferred_...  136 us
    all_gather x1, waiting for transfers between devices, body(): gathered = lax.all_gather(spectrum, 'px', axis=2, tiled=True)  123 us
    all_to_all x1, waiting for transfers between devices, body(): lax.all_to_all(along_z, 'px', split_axis=2, concat_axis=3, tiled=True)  90.6 us
    all_to_all x1, waiting for transfers between devices, body(): lax.all_to_all(planes, 'px', split_axis=3, concat_axis=2, tiled=True)  76.2 us
    unnamed x18, local copies, waits for them, and re-layouts  56.6 us
    unnamed x3, other arithmetic  39.1 us
    all_to_all x1, blocking collectives, body(): lax.all_to_all(jnp.stack([back_real, back_imag], axis=0), 'py', split_axi...  28.6 us
    all_to_all x2, local copies, waits for them, and re-layouts, body(): lax.all_to_all(planes, 'px', split_axis=3, concat_axis=2, tiled=True)  28.2 us
  transfers between devices with their start and end apart: 3, of which 3 were waited for; matrix products, arithmetic and copies ran while one was open for 2% of the time, Pallas kernels for 0%

commit v1 on v0

--- a/solution.py
+++ b/solution.py
@@ -3,7 +3,10 @@
 
 import jax
 import jax.numpy as jnp
+import numpy as np
 from jax import lax
+from jax.experimental import pallas as pl
+from jax.experimental.pallas import tpu as pltpu
 from jax.sharding import PartitionSpec as P
 
 MX = 64
@@ -42,7 +45,7 @@
     return contract("pbcxky,pkz->bcxyz", piece, table)
 
 
-def body(field, spectral_weight, point_weight, point_bias):
+def plain_body(field, spectral_weight, point_weight, point_bias):
     batch, channels, rows_x, rows_y, depth = field.shape
     grid_x = rows_x * lax.axis_size("px")
     grid_y = rows_y * lax.axis_size("py")
@@ -120,6 +123,377 @@
     return jax.nn.gelu(spectral + pointwise, approximate=False).astype(jnp.bfloat16)
 
 
+BF = jnp.bfloat16
+F32 = jnp.float32
+VMEM = pltpu.VMEM
+LANES = 128
+
+
+def signed_numbers(count):
+    number = np.arange(count)
+    return np.where(number < count // 2, number, number - count)
+
+
+def angles(length, positions, numbers):
+    return 2.0 * np.pi * (np.multiply.outer(positions, numbers) % length) / length
+
+
+def constant(table):
+    return jnp.asarray(np.asarray(table, np.float32), BF)
+
+
+def whole(shape):
+    return pl.BlockSpec(shape, lambda i: (0,) * len(shape))
+
+
+def greet(axis, me, n):
+    barrier = pltpu.get_barrier_semaphore()
+    for k in range(1, n):
+        pl.semaphore_signal(
+            barrier, inc=1, device_id={axis: lax.rem(me + k, n)},
+            device_id_type=pl.DeviceIdType.MESH,
+        )
+    pl.semaphore_wait(barrier, n - 1)
+
+
+def exchange_kernel(axis, n, x_ref, o_ref, send_sem, recv_sem, own_sem):
+    me = lax.axis_index(axis)
+    greet(axis, me, n)
+    copies = []
+    for k in range(1, n):
+        peer = lax.rem(me + k, n)
+        copy = pltpu.make_async_remote_copy(
+            src_ref=x_ref.at[peer], dst_ref=o_ref.at[me],
+            send_sem=send_sem.at[k], recv_sem=recv_sem.at[k],
+            device_id={axis: peer}, device_id_type=pl.DeviceIdType.MESH,
+        )
+        copy.start()
+        copies.append(copy)
+    own = pltpu.make_async_copy(x_ref.at[me], o_ref.at[me], own_sem)
+    own.start()
+    own.wait()
+    for copy in copies:
+        copy.wait()
+
+
+def exchange(x, axis, n, number):
+    return pl.pallas_call(
+        partial(exchange_kernel, axis, n),
+        out_shape=jax.ShapeDtypeStruct(x.shape, x.dtype),
+        in_specs=[pl.BlockSpec(memory_space=VMEM)],
+        out_specs=pl.BlockSpec(memory_space=VMEM),
+        scratch_shapes=[
+            pltpu.SemaphoreType.DMA((n,)), pltpu.SemaphoreType.DMA((n,)), pltpu.SemaphoreType.DMA
+        ],
+        compiler_params=pltpu.CompilerParams(collective_id=number, has_side_effects=True),
+        name=f"exchange_{axis}_{number}",
+    )(x)
+
+
+def gather_kernel(axis, n, x_ref, o_ref, up_send, up_recv, down_send, down_recv, side_send, side_recv, own_sem):
+    me = lax.axis_index(axis)
+    rows = n // 2
+    h = me // 2
+    s = me % 2
+    greet(axis, me, n)
+
+    def copy_to(source_row, first, send, recv, peer):
+        place = source_row * 2 + s
+        return pltpu.make_async_remote_copy(
+            src_ref=x_ref if first else o_ref.at[place], dst_ref=o_ref.at[place],
+            send_sem=send, recv_sem=recv,
+            device_id={axis: peer}, device_id_type=pl.DeviceIdType.MESH,
+        )
+
+    def up(d):
+        return copy_to(h - d, d == 0, up_send.at[d], up_recv.at[d], me + 2)
+
+    def down(d):
+        return copy_to(h + d, d == 0, down_send.at[d], down_recv.at[d], me - 2)
+
+    def side(row, first):
+        return copy_to(row, first, side_send.at[row], side_recv.at[row], h * 2 + 1 - s)
+
+    def arrived(row, recv):
+        place = row * 2 + s
+        pltpu.make_async_remote_copy(
+            src_ref=o_ref.at[place], dst_ref=o_ref.at[place], send_sem=own_sem, recv_sem=recv,
+            device_id={axis: h * 2 + 1 - s}, device_id_type=pl.DeviceIdType.MESH,
+        ).wait_recv()
+
+    pl.when(h < rows - 1)(lambda: up(0).start())
+    pl.when(h > 0)(lambda: down(0).start())
+    side(h, True).start()
+    own = pltpu.make_async_copy(x_ref, o_ref.at[me], own_sem)
+    own.start()
+    own.wait()
+    for d in range(1, rows):
+
+        @pl.when(h - d >= 0)
+        def _():
+            arrived(h - d, up_recv.at[d - 1])
+            pl.when(h < rows - 1)(lambda: up(d).start())
+            side(h - d, False).start()
+
+        @pl.when(h + d <= rows - 1)
+        def _():
+            arrived(h + d, down_recv.at[d - 1])
+            pl.when(h > 0)(lambda: down(d).start())
+            side(h + d, False).start()
+
+    for row in range(rows):
+        pltpu.make_async_remote_copy(
+            src_ref=o_ref.at[row * 2 + 1 - s], dst_ref=o_ref.at[row * 2 + 1 - s],
+            send_sem=side_send.at[row], recv_sem=side_recv.at[row],
+            device_id={axis: h * 2 + 1 - s}, device_id_type=pl.DeviceIdType.MESH,
+        ).wait()
+    for d in range(rows):
+        pl.when((h - d >= 0) & (h < rows - 1))(lambda: up(d).wait_send())
+        pl.when((h + d <= rows - 1) & (h > 0))(lambda: down(d).wait_send())
+
+
+def gather(x, axis, n, number):
+    rows = n // 2
+    return pl.pallas_call(
+        partial(gather_kernel, axis, n),
+        out_shape=jax.ShapeDtypeStruct((n,) + x.shape, x.dtype),
+        in_specs=[pl.BlockSpec(memory_space=VMEM)],
+        out_specs=pl.BlockSpec(memory_space=VMEM),
+        scratch_shapes=[pltpu.SemaphoreType.DMA((rows,))] * 6 + [pltpu.SemaphoreType.DMA],
+        compiler_params=pltpu.CompilerParams(collective_id=number, has_side_effects=True),
+        name="gather",
+    )(x)
+
+
+def forward_z_kernel(f_ref, t_ref, o_ref):
+    parts, tiles, kept, lanes = o_ref.shape
+    r = lax.dot_general(t_ref[...], f_ref[...], (((1,), (1,)), ((), ())), preferred_element_type=F32)
+    r = r.astype(BF)
+    for q in range(parts):
+        for t in range(tiles):
+            o_ref[q, t] = r[q * kept:(q + 1) * kept, t * lanes:(t + 1) * lanes]
+
+
+def forward_y_kernel(a_ref, t_ref, o_ref):
+    parts, tiles, kept, lanes = a_ref.shape
+    left = jnp.concatenate([a_ref[q].reshape(tiles * kept, lanes) for q in range(parts)], axis=1)
+    r = jnp.dot(left, t_ref[...], preferred_element_type=F32)
+    half = r.shape[1] // 2
+    r = r.reshape(tiles, 2, kept // 2, 2 * half)
+    r = r[:, 0, :, :half] + r[:, 1, :, half:]
+    o_ref[...] = r.reshape(o_ref.shape).astype(BF)
+
+
+def forward_x_kernel(a_ref, t_ref, o_ref):
+    depth = o_ref.shape[1]
+    v = a_ref[...].astype(F32)
+    blocks, rows, wide = v.shape
+    v = v.reshape(blocks * rows // depth, depth, wide)
+    pieces = [
+        jnp.swapaxes(v[:, :, g * LANES:(g + 1) * LANES], 0, 1) for g in range(wide // LANES)
+    ]
+    stacked = jnp.concatenate(pieces, axis=1).astype(BF)
+    lane = lax.broadcasted_iota(jnp.int32, (MX, LANES), 1)
+    for l in range(depth):
+        r = jnp.dot(t_ref[...], stacked[l], preferred_element_type=F32)
+        turned = pltpu.roll(r[MX:], MY, 1)
+        o_ref[0, l] = (r[:MX] + jnp.where(lane < MY, turned, -turned)).astype(BF)
+
+
+def mix_kernel(s_ref, w_ref, t_ref, o_ref, held):
+    channels, depth = s_ref.shape[:2]
+
+    def one(l, carry):
+        real = jnp.zeros((MX, MY), F32)
+        imag = jnp.zeros((MX, MY), F32)
+        for c in range(channels):
+            s = s_ref[c, l].astype(F32)
+            s_real, s_imag = s[:, :MY], s[:, MY:]
+            w_real = w_ref[0, c, 0, l].astype(F32)
+            w_imag = w_ref[1, c, 0, l].astype(F32)
+            real = real + (s_real * w_real - s_imag * w_imag)
+            imag = imag + (s_real * w_imag + s_imag * w_real)
+        both = jnp.concatenate([real, imag], axis=1)
+        turned = jnp.concatenate([-imag, real], axis=1)
+        stacked = jnp.concatenate([both, turned], axis=0).astype(BF)
+        held[l] = jnp.dot(t_ref[...], stacked, preferred_element_type=F32)
+        return carry
+
+    lax.fori_loop(0, depth, one, 0)
+    blocks, rows, wide = o_ref.shape
+    count = wide // LANES
+    step = held.shape[1] // count
+    for g in range(count):
+        v = jnp.swapaxes(held[:, g * step:(g + 1) * step, :], 0, 1)
+        o_ref[:, :, g * LANES:(g + 1) * LANES] = v.reshape(blocks, rows, LANES).astype(BF)
+
+
+def inverse_y_kernel(a_ref, t_ref, o_ref):
+    parts, tiles, kept, lanes = o_ref.shape
+    r = jnp.dot(a_ref[0], t_ref[...], preferred_element_type=F32)
+    r = r.reshape(tiles, kept // 2, r.shape[1])
+    for q in range(parts):
+        first = 2 * q * lanes
+        o_ref[q] = jnp.concatenate(
+            [r[:, :, first:first + lanes], r[:, :, first + lanes:first + 2 * lanes]], axis=1
+        ).astype(BF)
+
+
+def final_kernel(a_ref, f_ref, t_ref, k_ref, b_ref, o_ref, held):
+    parts, channels = a_ref.shape[:2]
+    rows = f_ref.shape[1]
+    depth = f_ref.shape[2]
+
+    def one(o, carry):
+        left = jnp.concatenate([a_ref[q, o, 0] for q in range(parts)], axis=0)
+        held[o] = lax.dot_general(
+            left, t_ref[...], (((0,), (0,)), ((), ())), preferred_element_type=F32
+        )
+        return carry
+
+    lax.fori_loop(0, channels, one, 0, unroll=4)
+    sub = k_ref.shape[0] // channels
+
+    def two(r, carry):
+        spot = pl.ds(pl.multiple_of(r * sub, sub), sub)
+        f = f_ref[:, spot, :].reshape(channels * sub, depth)
+        v = jnp.dot(k_ref[...], f, preferred_element_type=F32) + b_ref[...]
+        v = v + held[:, spot, :].reshape(channels * sub, depth)
+        v = 0.5 * v * (1.0 + lax.erf(v * math.sqrt(0.5)))
+        o_ref[:, spot, :] = v.reshape(channels, sub, depth).astype(BF)
+        return carry
+
+    lax.fori_loop(0, rows // sub, two, 0)
+
+
+def body(field, spectral_weight, point_weight, point_bias):
+    batch, channels, rows_x, rows_y, depth = field.shape
+    n_p = lax.axis_size("px")
+    n_q = lax.axis_size("py")
+    group = max(1, LANES // rows_y)
+    own_l = MZ // n_q
+    own_c = channels // n_p
+    if (
+        batch != 1 or group * rows_y != LANES or rows_x % group or own_l % 8
+        or channels % n_p or n_p % 2 or 2 * MY != LANES
+    ):
+        return plain_body(field, spectral_weight, point_weight, point_bias)
+    grid_x, grid_y = rows_x * n_p, rows_y * n_q
+    tiles_x = rows_x // group
+    tiles = channels * tiles_x
+    kept = 2 * own_l
+    wide = group * LANES
+    steps = n_p
+    per_step = tiles // steps
+
+    theta = angles(depth, np.arange(depth), np.arange(MZ))
+    table_z = np.stack([np.cos(theta), -np.sin(theta)]).reshape(2, depth, n_q, own_l)
+    table_z = table_z.transpose(2, 0, 3, 1).reshape(n_q * kept, depth)
+    weight = np.where(np.arange(MZ) == 0, 1.0, 2.0) / float(grid_x * grid_y * depth)
+    back_z = np.stack([np.cos(theta) * weight, -np.sin(theta) * weight])
+    back_z = back_z.reshape(2, depth, n_q, own_l).transpose(2, 0, 3, 1).reshape(n_q * kept, depth)
+
+    theta = angles(grid_y, np.arange(grid_y), signed_numbers(MY))
+    cos_y, sin_y = np.cos(theta), np.sin(theta)
+    eye = np.eye(group)
+    rule = np.stack([np.stack([cos_y, -sin_y], 1), np.stack([sin_y, cos_y], 1)])
+    rule = rule.reshape(2, n_q, rows_y, 2, MY)
+    table_y = np.einsum("uqyrj,gh->qgyuhrj", rule, eye).reshape(n_q * LANES, 2 * wide)
+    rule = np.stack([np.stack([cos_y, sin_y]), np.stack([-sin_y, cos_y])])
+    rule = rule.reshape(2, 2, n_q, rows_y, MY)
+    back_y = np.einsum("urqyj,gh->gujqrhy", rule, eye).reshape(wide, 2 * n_q * LANES)
+
+    order = np.arange(grid_x).reshape(n_p * tiles_x, group).T.reshape(-1)
+    theta = angles(grid_x, order, signed_numbers(MX))
+    table_x = np.concatenate([np.cos(theta).T, np.sin(theta).T], axis=0)
+    back_x = np.concatenate([np.cos(theta), np.sin(theta)], axis=1)
+
+    along_z = pl.pallas_call(
+        forward_z_kernel,
+        grid=(steps,),
+        in_specs=[
+            pl.BlockSpec((per_step * LANES, depth), lambda i: (i, 0)),
+            whole(table_z.shape),
+        ],
+        out_specs=pl.BlockSpec((n_q, per_step, kept, LANES), lambda i: (0, i, 0, 0)),
+        out_shape=jax.ShapeDtypeStruct((n_q, tiles, kept, LANES), BF),
+        name="forward_z",
+    )(field.reshape(tiles * LANES, depth), constant(table_z))
+    along_z = exchange(along_z, "py", n_q, 1)
+    along_y = pl.pallas_call(
+        forward_y_kernel,
+        grid=(steps,),
+        in_specs=[
+            pl.BlockSpec((n_q, per_step, kept, LANES), lambda i: (0, i, 0, 0)),
+            whole(table_y.shape),
+        ],
+        out_specs=pl.BlockSpec((1, per_step * own_l, wide), lambda i: (i, 0, 0)),
+        out_shape=jax.ShapeDtypeStruct((n_p, per_step * own_l, wide), BF),
+        name="forward_y",
+    )(along_z, constant(table_y))
+    along_y = exchange(along_y, "px", n_p, 2)
+    spectrum = pl.pallas_call(
+        forward_x_kernel,
+        grid=(own_c,),
+        in_specs=[
+            pl.BlockSpec((n_p, tiles_x * own_l, wide), lambda i: (0, i, 0)),
+            whole(table_x.shape),
+        ],
+        out_specs=pl.BlockSpec((1, own_l, MX, LANES), lambda i: (i, 0, 0, 0)),
+        out_shape=jax.ShapeDtypeStruct((own_c, own_l, MX, LANES), BF),
+        name="forward_x",
+    )(along_y, constant(table_x))
+    spectrum = gather(spectrum, "px", n_p, 3).reshape(channels, own_l, MX, LANES)
+    mixed = pl.pallas_call(
+        mix_kernel,
+        grid=(own_c,),
+        in_specs=[
+            whole(spectrum.shape),
+            pl.BlockSpec((2, channels, 1, own_l, MX, MY), lambda i: (0, 0, i, 0, 0, 0)),
+            whole(back_x.shape),
+        ],
+        out_specs=pl.BlockSpec((n_p, tiles_x * own_l, wide), lambda i: (0, i, 0)),
+        out_shape=jax.ShapeDtypeStruct((n_p, own_c * tiles_x * own_l, wide), BF),
+        scratch_shapes=[pltpu.VMEM((own_l, grid_x, LANES), F32)],
+        name="mix",
+    )(spectrum, spectral_weight, constant(back_x))
+    mixed = exchange(mixed, "px", n_p, 4)
+    planes = pl.pallas_call(
+        inverse_y_kernel,
+        grid=(steps,),
+        in_specs=[
+            pl.BlockSpec((1, per_step * own_l, wide), lambda i: (i, 0, 0)),
+            whole(back_y.shape),
+        ],
+        out_specs=pl.BlockSpec((n_q, per_step, kept, LANES), lambda i: (0, i, 0, 0)),
+        out_shape=jax.ShapeDtypeStruct((n_q, tiles, kept, LANES), BF),
+        name="inverse_y",
+    )(mixed, constant(back_y))
+    planes = exchange(planes, "py", n_q, 5)
+    planes = planes.reshape(n_q, channels, tiles_x, kept, LANES)
+    sub = 16
+    spread = (
+        point_weight[:, None, :, None] * jnp.eye(sub, dtype=BF)[None, :, None, :]
+    ).reshape(channels * sub, channels * sub)
+    bias = jnp.repeat(point_bias, sub)[:, None]
+    out = pl.pallas_call(
+        final_kernel,
+        grid=(tiles_x,),
+        in_specs=[
+            pl.BlockSpec((n_q, channels, 1, kept, LANES), lambda i: (0, 0, i, 0, 0)),
+            pl.BlockSpec((channels, LANES, depth), lambda i: (0, i, 0)),
+            whole(back_z.shape),
+            whole(spread.shape),
+            whole(bias.shape),
+        ],
+        out_specs=pl.BlockSpec((channels, LANES, depth), lambda i: (0, i, 0)),
+        out_shape=jax.ShapeDtypeStruct((channels, rows_x * rows_y, depth), BF),
+        scratch_shapes=[pltpu.VMEM((channels, LANES, depth), F32)],
+        name="final",
+    )(planes, field.reshape(channels, rows_x * rows_y, depth), constant(back_z), spread, bias)
+    return out.reshape(field.shape)
+
+
 def solution(mesh):
     placed = (P(None, None, "px", "py", None), P(None, None, "px", "py", None, None), P(), P())
     return jax.shard_map(

time: 756 us -> 365 us (0.48); the launches traced: 741 us -> 364 us
  Pallas kernels: 0 us -> 352 us
  waiting for transfers between devices: 290 us -> 0 us
  matrix products: 150 us -> 0 us
  local copies, waits for them, and re-layouts: 139 us -> 9.99 us
  other arithmetic: 78.1 us -> 2.36 us
  blocking collectives: 56.2 us -> 0 us
  between operations: 14.2 us -> 0.06 us
  starting transfers between devices: 13.4 us -> 0 us
    pallas_call x0 -> x11, Pallas kernels: none -> 352 us  [the longest x1 135 us: body(): pl.pallas_call(mix_kernel, grid=(own_c,), in_specs=[whole(spectrum.shape)...]
    all_to_all x2 -> x0, waiting for transfers between devices: 167 us -> none  [the longest x1 90.6 us: body(): lax.all_to_all(along_z, 'px', split_axis=2, concat_axis=3, tiled=True)]
    dot_general x20 -> x0, matrix products: 150 us -> none  [the longest x19 136 us: contract(): jnp.einsum(form, left, right, precision=lax.Precision.HIGHEST, preferred_...]
    all_gather x1 -> x0, waiting for transfers between devices: 123 us -> none  [body(): gathered = lax.all_gather(spectrum, 'px', axis=2, tiled=True)]
    unnamed x18 -> x2, local copies, waits for them, and re-layouts: 56.6 us -> 0.01 us
    all_to_all x2 -> x0, blocking collectives: 56.2 us -> none  [the longest x1 28.6 us: body(): lax.all_to_all(jnp.stack([back_real, back_imag], axis=0), 'py', split_axi...]
    unnamed x3 -> x0, other arithmetic: 39.1 us -> none
    all_to_all x6 -> x0, local copies, waits for them, and re-layouts: 38.7 us -> none  [the longest x2 28.2 us: body(): lax.all_to_all(planes, 'px', split_axis=3, concat_axis=2, tiled=True)]
  transfers between devices with their start and end apart: 3 -> 0, of which waited for: 3 -> 0; matrix products, arithmetic and copies ran while one was open for 2% -> 0% of each run, Pallas kernels for 0% -> 0%
where the time goes in v1:
time: 365 us; the launch traced here: 364 us
  Pallas kernels  352 us (96%)
  local copies, waits for them, and re-layouts  9.99 us (3%)
    pallas_call x1, Pallas kernels, body(): pl.pallas_call(mix_kernel, grid=(own_c,), in_specs=[whole(spectrum.shape)...  135 us
    pallas_call x4, Pallas kernels, exchange(): pl.pallas_call(partial(exchange_kernel, axis, n), out_shape=jax.ShapeDtyp...  114 us
    pallas_call x1, Pallas kernels, gather(): pl.pallas_call(partial(gather_kernel, axis, n), out_shape=jax.ShapeDtypeS...  53.6 us
    pallas_call x1, Pallas kernels, body(): pl.pallas_call(final_kernel, grid=(tiles_x,), in_specs=[pl.BlockSpec((n_q...  21.9 us
    pallas_call x1, Pallas kernels, body(): pl.pallas_call(forward_z_kernel, grid=(steps,), in_specs=[pl.BlockSpec((p...  8.52 us
    mul x1, local copies, waits for them, and re-layouts, body(): point_weight[:, None, :, None] * jnp.eye(sub, dtype=BF)[None, :, None, :]  8.4 us
    pallas_call x1, Pallas kernels, body(): pl.pallas_call(forward_y_kernel, grid=(steps,), in_specs=[pl.BlockSpec((n...  7.45 us

profile of v1, /device:TPU:15, one launch (start us, length us, event | category | flops | bytes accessed | tf_op | source)
XLA Modules:
  0.0 364.3 jit_solution(13743267313410986179)
XLA Ops:
  0.0 0.7 broadcast_in_dim.2
  0.7 0.9 broadcast_in_dim_reshape.4.b_ref
  1.6 8.5 %forward_z.1.x_ref = bf16[4,128,16,128]{3,2,1,0:T(8,128)(2,1)} custom-call(bf16[16384,256]{1,0:T(8,128)(2,1)} %bitcast.7, bf16[64,256]{1,0:T(8,128)(2,1)} %constant.12.clone.t_ref), custom_call_target="tpu_custom_call" | custom-call | tf_op jit(solution)/shard_map/forward_z/pallas_call | solution.py:411
  10.1 28.5 %exchange_py_1.1.a_ref = bf16[4,128,16,128]{3,2,1,0:T(8,128)(2,1)} custom-call(bf16[4,128,16,128]{3,2,1,0:T(8,128)(2,1)} %forward_z.1.x_ref), custom_call_target="tpu_custom_call" | custom-call | tf_op jit(solution)/shard_map/exchange_py_1/pallas_call | solution.py:180
  38.6 7.5 %forward_y.1.x_ref = bf16[8,128,512]{2,1,0:T(8,128)(2,1)} custom-call(bf16[4,128,16,128]{3,2,1,0:T(8,128)(2,1)} %exchange_py_1.1.a_ref, bf16[512,1024]{1,0:T(8,128)(2,1)} %constant.13.clone.t_ref), custom_call_target="tpu_custom_call" | custom-call | tf_op jit(solution)/shard_map/forward_y/pallas_call | solution.py:423
  46.0 28.7 %exchange_px_2.1.a_ref = bf16[8,128,512]{2,1,0:T(8,128)(2,1)} custom-call(bf16[8,128,512]{2,1,0:T(8,128)(2,1)} %forward_y.1.x_ref), custom_call_target="tpu_custom_call" | custom-call | tf_op jit(solution)/shard_map/exchange_px_2/pallas_call | solution.py:180
  74.8 4.0 %forward_x.1.x_ref = bf16[4,8,64,128]{3,2,1,0:T(8,128)(2,1)} custom-call(bf16[8,128,512]{2,1,0:T(8,128)(2,1)} %exchange_px_2.1.a_ref, bf16[128,128]{1,0:T(8,128)(2,1)} %constant.14.clone.t_ref), custom_call_target="tpu_custom_call" | custom-call | tf_op jit(solution)/shard_map/forward_x/pallas_call | solution.py:435
  78.8 53.6 %gather.1 = bf16[8,4,8,64,128]{4,3,2,1,0:T(8,128)(2,1)} custom-call(bf16[4,8,64,128]{3,2,1,0:T(8,128)(2,1)} %forward_x.1.x_ref), custom_call_target="tpu_custom_call" | custom-call | tf_op jit(solution)/shard_map/gather/pallas_call | solution.py:257
  132.4 135.2 %mix.1.x_ref = bf16[8,128,512]{2,1,0:T(8,128)(2,1)} custom-call(bf16[32,8,64,128]{3,2,1,0:T(8,128)(2,1)} %bitcast.9, bf16[2,32,4,8,64,64]{5,4,3,2,1,0:T(8,128)(2,1)} %w_ref.1, bf16[128,128]{1,0:T(8,128)(2,1)} %constant.15.clone.t_ref), custom_call_target="tpu_custom_call" | custom-call | tf_op jit(solution)/shard_map/mix/pallas_call | solution.py:447
  267.6 27.9 %exchange_px_4.1.a_ref = bf16[8,128,512]{2,1,0:T(8,128)(2,1)} custom-call(bf16[8,128,512]{2,1,0:T(8,128)(2,1)} %mix.1.x_ref), custom_call_target="tpu_custom_call" | custom-call | tf_op jit(solution)/shard_map/exchange_px_4/pallas_call | solution.py:180
  295.4 0.0 copy-start
  295.4 7.0 %inverse_y.1.x_ref = bf16[4,128,16,128]{3,2,1,0:T(8,128)(2,1)} custom-call(bf16[8,128,512]{2,1,0:T(8,128)(2,1)} %exchange_px_4.1.a_ref, bf16[512,1024]{1,0:T(8,128)(2,1)} %constant.16.clone.t_ref), custom_call_target="tpu_custom_call" | custom-call | tf_op jit(solution)/shard_map/inverse_y/pallas_call | solution.py:461
  302.4 29.2 %exchange_py_5.1 = bf16[4,128,16,128]{3,2,1,0:T(8,128)(2,1)} custom-call(bf16[4,128,16,128]{3,2,1,0:T(8,128)(2,1)} %inverse_y.1.x_ref), custom_call_target="tpu_custom_call" | custom-call | tf_op jit(solution)/shard_map/exchange_py_5/pallas_call | solution.py:180
  331.6 0.0 copy-done
  331.6 2.4 broadcast_multiply_fusion
  334.0 8.4 %mul.20.k_ref = bf16[512,512]{1,0:T(8,128)(2,1)} reshape(bf16[32,16,32,16]{3,2,1,0:T(8,128)(2,1)} %broadcast_multiply_fusion) | data formatting | bytes 1048576 | tf_op jit(solution)/shard_map/mul | solution.py:476
  342.4 21.9 %final.1 = bf16[32,512,256]{2,1,0:T(8,128)(2,1)} custom-call(bf16[4,32,4,16,128]{4,3,2,1,0:T(8,128)(2,1)} %bitcast.10, bf16[32,512,256]{2,1,0:T(8,128)(2,1)} %bitcast.8, bf16[64,256]{1,0:T(8,128)(2,1)} %constant.17.clone.t_ref, bf16[512,512]{1,0:T(8,128)(2,1)} %mul.20.k_ref, f32[512,1]{1,0:T(8,128)} %broadcast_in_dim_reshape.4.b_ref), custom_call_target="tpu_custom_call" | custom-call | tf_op jit(solution)/shard_map/final/pallas_call | solution.py:479
  (1 shorter events, 0.0 us)
Async XLA Ops:
  295.4 36.2 %copy-start = (bf16[32,32]{1,0:T(8,128)(2,1)S(1)}, bf16[32,32]{1,0:T(8,128)(2,1)}, u32[]{:S(2)}) copy-start(bf16[32,32]{1,0:T(8,128)(2,1)} %param.12) | copy-start | bytes 6148

commit v2 on v1

--- a/solution.py
+++ b/solution.py
@@ -300,21 +300,42 @@
         o_ref[0, l] = (r[:MX] + jnp.where(lane < MY, turned, -turned)).astype(BF)
 
 
-def mix_kernel(s_ref, w_ref, t_ref, o_ref, held):
+def mix_kernel(s_ref, w_ref, t_ref, o_ref, held, twin, total):
     channels, depth = s_ref.shape[:2]
+    strip = 32
+
+    @pl.when(pl.program_id(0) == 0)
+    def _():
+        def double(c, carry):
+            for l in range(depth):
+                s = s_ref[c, l]
+                twin[0, c, l] = jnp.concatenate([s[:, :MY], s[:, :MY]], axis=1)
+                twin[1, c, l] = jnp.concatenate([s[:, MY:], s[:, MY:]], axis=1)
+            return carry
+
+        lax.fori_loop(0, channels, double, 0)
 
     def one(l, carry):
-        real = jnp.zeros((MX, MY), F32)
-        imag = jnp.zeros((MX, MY), F32)
-        for c in range(channels):
-            s = s_ref[c, l].astype(F32)
-            s_real, s_imag = s[:, :MY], s[:, MY:]
-            w_real = w_ref[0, c, 0, l].astype(F32)
-            w_imag = w_ref[1, c, 0, l].astype(F32)
-            real = real + (s_real * w_real - s_imag * w_imag)
-            imag = imag + (s_real * w_imag + s_imag * w_real)
-        both = jnp.concatenate([real, imag], axis=1)
-        turned = jnp.concatenate([-imag, real], axis=1)
+        def piece(k, inner):
+            spot = pl.ds(pl.multiple_of(k * strip, strip), strip)
+            first = jnp.zeros((strip, LANES), F32)
+            second = jnp.zeros((strip, LANES), F32)
+            for c in range(channels):
+                w = jnp.concatenate(
+                    [w_ref[0, c, 0, l, spot, :], w_ref[1, c, 0, l, spot, :]], axis=1
+                ).astype(F32)
+                first = first + twin[0, c, l, spot, :].astype(F32) * w
+                second = second + twin[1, c, l, spot, :].astype(F32) * w
+            total[0, spot, :] = first
+            total[1, spot, :] = second
+            return inner
+
+        lax.fori_loop(0, MX // strip, piece, 0)
+        lane = lax.broadcasted_iota(jnp.int32, (MX, LANES), 1)
+        second = pltpu.roll(total[1], MY, 1)
+        both = total[0] + jnp.where(lane < MY, -second, second)
+        turned = pltpu.roll(both, MY, 1)
+        turned = jnp.where(lane < MY, -turned, turned)
         stacked = jnp.concatenate([both, turned], axis=0).astype(BF)
         held[l] = jnp.dot(t_ref[...], stacked, preferred_element_type=F32)
         return carry
@@ -339,25 +360,35 @@
         ).astype(BF)
 
 
-def final_kernel(a_ref, f_ref, t_ref, k_ref, b_ref, o_ref, held):
+def final_kernel(a_ref, f_ref, t_ref, e_ref, p_ref, b_ref, o_ref, held, k_ref):
     parts, channels = a_ref.shape[:2]
     rows = f_ref.shape[1]
     depth = f_ref.shape[2]
+    sub = k_ref.shape[0] // channels
+
+    @pl.when(pl.program_id(0) == 0)
+    def _():
+        tall = jnp.dot(e_ref[...], p_ref[...], preferred_element_type=F32).astype(BF)
+        full = lax.dot_general(
+            tall, e_ref[...], (((1,), (1,)), ((), ())), preferred_element_type=F32
+        )
+        row = lax.broadcasted_iota(jnp.int32, full.shape, 0)
+        column = lax.broadcasted_iota(jnp.int32, full.shape, 1)
+        k_ref[...] = jnp.where(row % sub == column % sub, full, 0.0).astype(BF)
 
     def one(o, carry):
         left = jnp.concatenate([a_ref[q, o, 0] for q in range(parts)], axis=0)
         held[o] = lax.dot_general(
             left, t_ref[...], (((0,), (0,)), ((), ())), preferred_element_type=F32
-        )
+        ) + b_ref[o]
         return carry
 
     lax.fori_loop(0, channels, one, 0, unroll=4)
-    sub = k_ref.shape[0] // channels
 
     def two(r, carry):
         spot = pl.ds(pl.multiple_of(r * sub, sub), sub)
         f = f_ref[:, spot, :].reshape(channels * sub, depth)
-        v = jnp.dot(k_ref[...], f, preferred_element_type=F32) + b_ref[...]
+        v = jnp.dot(k_ref[...], f, preferred_element_type=F32)
         v = v + held[:, spot, :].reshape(channels * sub, depth)
         v = 0.5 * v * (1.0 + lax.erf(v * math.sqrt(0.5)))
         o_ref[:, spot, :] = v.reshape(channels, sub, depth).astype(BF)
@@ -454,7 +485,11 @@
         ],
         out_specs=pl.BlockSpec((n_p, tiles_x * own_l, wide), lambda i: (0, i, 0)),
         out_shape=jax.ShapeDtypeStruct((n_p, own_c * tiles_x * own_l, wide), BF),
-        scratch_shapes=[pltpu.VMEM((own_l, grid_x, LANES), F32)],
+        scratch_shapes=[
+            pltpu.VMEM((own_l, grid_x, LANES), F32),
+            pltpu.VMEM((2,) + spectrum.shape, BF),
+            pltpu.VMEM((2, MX, LANES), F32),
+        ],
         name="mix",
     )(spectrum, spectral_weight, constant(back_x))
     mixed = exchange(mixed, "px", n_p, 4)
@@ -472,10 +507,7 @@
     planes = exchange(planes, "py", n_q, 5)
     planes = planes.reshape(n_q, channels, tiles_x, kept, LANES)
     sub = 16
-    spread = (
-        point_weight[:, None, :, None] * jnp.eye(sub, dtype=BF)[None, :, None, :]
-    ).reshape(channels * sub, channels * sub)
-    bias = jnp.repeat(point_bias, sub)[:, None]
+    spread = np.repeat(np.eye(channels), sub, axis=0)
     out = pl.pallas_call(
         final_kernel,
         grid=(tiles_x,),
@@ -484,13 +516,20 @@
             pl.BlockSpec((channels, LANES, depth), lambda i: (0, i, 0)),
             whole(back_z.shape),
             whole(spread.shape),
-            whole(bias.shape),
+            whole(point_weight.shape),
+            pl.BlockSpec(memory_space=pltpu.SMEM),
         ],
         out_specs=pl.BlockSpec((channels, LANES, depth), lambda i: (0, i, 0)),
         out_shape=jax.ShapeDtypeStruct((channels, rows_x * rows_y, depth), BF),
-        scratch_shapes=[pltpu.VMEM((channels, LANES, depth), F32)],
+        scratch_shapes=[
+            pltpu.VMEM((channels, LANES, depth), F32),
+            pltpu.VMEM((channels * sub, channels * sub), BF),
+        ],
         name="final",
-    )(planes, field.reshape(channels, rows_x * rows_y, depth), constant(back_z), spread, bias)
+    )(
+        planes, field.reshape(channels, rows_x * rows_y, depth), constant(back_z),
+        constant(spread), point_weight, point_bias,
+    )
     return out.reshape(field.shape)
 
 

time: 365 us -> 244 us (0.67)
  Pallas kernels: 352 us -> 243 us
  local copies, waits for them, and re-layouts: 9.99 us -> 0 us
    pallas_call x1, Pallas kernels: 135 us -> 27 us  [body(): pl.pallas_call(mix_kernel, grid=(own_c,), in_specs=[whole(spectrum.shape)...]
    mul x1 -> x0, local copies, waits for them, and re-layouts: 8.4 us -> none  [body(): point_weight[:, None, :, None] * jnp.eye(sub, dtype=BF)[None, :, None, :]]
where the time goes in v2:
time: 244 us; the launch traced here: 243 us
  Pallas kernels  243 us (100%)
    pallas_call x4, Pallas kernels, exchange(): pl.pallas_call(partial(exchange_kernel, axis, n), out_shape=jax.ShapeDtyp...  114 us
    pallas_call x1, Pallas kernels, gather(): pl.pallas_call(partial(gather_kernel, axis, n), out_shape=jax.ShapeDtypeS...  53.5 us
    pallas_call x1, Pallas kernels, body(): pl.pallas_call(mix_kernel, grid=(own_c,), in_specs=[whole(spectrum.shape)...  27 us
    pallas_call x1, Pallas kernels, body(): pl.pallas_call(final_kernel, grid=(tiles_x,), in_specs=[pl.BlockSpec((n_q...  21.6 us
    pallas_call x1, Pallas kernels, body(): pl.pallas_call(forward_z_kernel, grid=(steps,), in_specs=[pl.BlockSpec((p...  8.52 us
    pallas_call x1, Pallas kernels, body(): pl.pallas_call(forward_y_kernel, grid=(steps,), in_specs=[pl.BlockSpec((n...  7.46 us
    pallas_call x1, Pallas kernels, body(): pl.pallas_call(inverse_y_kernel, grid=(steps,), in_specs=[pl.BlockSpec((1...  6.96 us

profile of v2, /device:TPU:15, one launch (start us, length us, event | category | flops | bytes accessed | tf_op | source)
XLA Modules:
  0.0 243.4 jit_solution(9240285784091029169)
XLA Ops:
  0.0 8.5 %forward_z.1.x_ref = bf16[4,128,16,128]{3,2,1,0:T(8,128)(2,1)} custom-call(bf16[16384,256]{1,0:T(8,128)(2,1)} %bitcast.5, bf16[64,256]{1,0:T(8,128)(2,1)} %constant.14.clone.t_ref), custom_call_target="tpu_custom_call" | custom-call | tf_op jit(solution)/shard_map/forward_z/pallas_call | solution.py:442
  8.5 28.5 %exchange_py_1.1.a_ref = bf16[4,128,16,128]{3,2,1,0:T(8,128)(2,1)} custom-call(bf16[4,128,16,128]{3,2,1,0:T(8,128)(2,1)} %forward_z.1.x_ref), custom_call_target="tpu_custom_call" | custom-call | tf_op jit(solution)/shard_map/exchange_py_1/pallas_call | solution.py:180
  37.0 7.5 %forward_y.1.x_ref = bf16[8,128,512]{2,1,0:T(8,128)(2,1)} custom-call(bf16[4,128,16,128]{3,2,1,0:T(8,128)(2,1)} %exchange_py_1.1.a_ref, bf16[512,1024]{1,0:T(8,128)(2,1)} %constant.15.clone.t_ref), custom_call_target="tpu_custom_call" | custom-call | tf_op jit(solution)/shard_map/forward_y/pallas_call | solution.py:454
  44.5 28.7 %exchange_px_2.1.a_ref = bf16[8,128,512]{2,1,0:T(8,128)(2,1)} custom-call(bf16[8,128,512]{2,1,0:T(8,128)(2,1)} %forward_y.1.x_ref), custom_call_target="tpu_custom_call" | custom-call | tf_op jit(solution)/shard_map/exchange_px_2/pallas_call | solution.py:180
  73.2 4.0 %forward_x.1.x_ref = bf16[4,8,64,128]{3,2,1,0:T(8,128)(2,1)} custom-call(bf16[8,128,512]{2,1,0:T(8,128)(2,1)} %exchange_px_2.1.a_ref, bf16[128,128]{1,0:T(8,128)(2,1)} %constant.16.clone.t_ref), custom_call_target="tpu_custom_call" | custom-call | tf_op jit(solution)/shard_map/forward_x/pallas_call | solution.py:466
  77.2 53.5 %gather.1 = bf16[8,4,8,64,128]{4,3,2,1,0:T(8,128)(2,1)} custom-call(bf16[4,8,64,128]{3,2,1,0:T(8,128)(2,1)} %forward_x.1.x_ref), custom_call_target="tpu_custom_call" | custom-call | tf_op jit(solution)/shard_map/gather/pallas_call | solution.py:257
  130.8 27.0 %mix.1.x_ref = bf16[8,128,512]{2,1,0:T(8,128)(2,1)} custom-call(bf16[32,8,64,128]{3,2,1,0:T(8,128)(2,1)} %bitcast.7, bf16[2,32,4,8,64,64]{5,4,3,2,1,0:T(8,128)(2,1)} %w_ref.1, bf16[128,128]{1,0:T(8,128)(2,1)} %constant.17.clone.t_ref), custom_call_target="tpu_custom_call" | custom-call | tf_op jit(solution)/shard_map/mix/pallas_call | solution.py:478
  157.7 27.9 %exchange_px_4.1.a_ref = bf16[8,128,512]{2,1,0:T(8,128)(2,1)} custom-call(bf16[8,128,512]{2,1,0:T(8,128)(2,1)} %mix.1.x_ref), custom_call_target="tpu_custom_call" | custom-call | tf_op jit(solution)/shard_map/exchange_px_4/pallas_call | solution.py:180
  185.6 7.0 %inverse_y.1.x_ref = bf16[4,128,16,128]{3,2,1,0:T(8,128)(2,1)} custom-call(bf16[8,128,512]{2,1,0:T(8,128)(2,1)} %exchange_px_4.1.a_ref, bf16[512,1024]{1,0:T(8,128)(2,1)} %constant.18.clone.t_ref), custom_call_target="tpu_custom_call" | custom-call | tf_op jit(solution)/shard_map/inverse_y/pallas_call | solution.py:496
  192.6 29.2 %exchange_py_5.1 = bf16[4,128,16,128]{3,2,1,0:T(8,128)(2,1)} custom-call(bf16[4,128,16,128]{3,2,1,0:T(8,128)(2,1)} %inverse_y.1.x_ref), custom_call_target="tpu_custom_call" | custom-call | tf_op jit(solution)/shard_map/exchange_py_5/pallas_call | solution.py:180
  221.7 21.6 %final.1 = bf16[32,512,256]{2,1,0:T(8,128)(2,1)} custom-call(bf16[4,32,4,16,128]{4,3,2,1,0:T(8,128)(2,1)} %bitcast.8, bf16[32,512,256]{2,1,0:T(8,128)(2,1)} %bitcast.6, bf16[64,256]{1,0:T(8,128)(2,1)} %constant.19.clone.t_ref, bf16[512,32]{1,0:T(8,128)(2,1)} %constant.20.clone.e_ref, bf16[32,32]{1,0:T(8,128)(2,1)} %p_ref.1, f32[32]{0:T(128)} %b_ref.1), custom_call_target="tpu_custom_call" | custom-call | tf_op jit(solution)/shard_map/final/pallas_call | solution.py:511
